TPU v7x, 32 devices: a whole 2x2x4 slice. The times are simulated.
32 devices in a mesh: rep: 2 (over y), own: 16 (over z, x, core).
Axes of the slice: x: 2, y: 2, z: 4, core: 2. Of those that a mesh axis runs over, the one named last changes fastest.
Arguments:
- values: float32 [262144, 128], P(('rep', 'own')), may hold values from -0.8 to 0.8
- key_ids: int32 [262144], P(('rep', 'own')), may hold values from 0 to 65535, as said below
- heavy_ids: int32 [2048], replicated, may hold values from 0 to 65535, as said below
- block_offsets: int32 [32, 16], P(('rep', 'own')), may hold values from 0 to 8191, as said below
- block_counts: int32 [32, 16], P(('rep', 'own')), may hold values from 8 to 64, as said below
Outputs:
- light_sums: float32 [65536, 128], P('own')
- heavy_sums: float32 [2048, 128], P('own')
Inputs may be any that keep to these rules, and one draw needn't show every extreme that they name: `key_ids`: an event in block o of a device has a key in o * 4096 to (o + 1) * 4096 - 1 that is not a heavy key; every event outside all blocks has a heavy key. `heavy_ids`: distinct keys. `block_offsets`: on each device the blocks lie in the order of o, do not meet, and end by position 8192. `block_counts`: at most 64; one owner gets exactly 64 from every device.
All inputs are finite; a program needn't handle non-finite values.
Results may differ from a plain program's by a relative error of at most 0.000075.
Values sent between devices are 32-bit elements; how exact they have to be, the bound alone decides.
A program may use at most 64 MiB of HBM per device.

v0:
```python
import math
import jax
import jax.numpy as jnp
from jax import lax
from jax.sharding import PartitionSpec as P

KEYS_DEV = 4096
CAP = 64


def key_sums(rows_in, row_keys, targets):
    slots = row_keys.shape[0]
    block_len = math.gcd(slots, 2048)
    count_blocks = slots // block_len
    rows_blocks = rows_in.reshape(count_blocks, block_len, rows_in.shape[1])
    keys_blocks = row_keys.reshape(count_blocks, block_len)

    def accumulate(running, pieces):
        rows_piece, keys_piece = pieces
        onehot = (targets[:, None] == keys_piece[None, :]).astype(jnp.float32)
        added = jnp.dot(
            onehot, rows_piece, precision=lax.Precision.HIGHEST, preferred_element_type=jnp.float32
        )
        return (running + added, None)

    start_sums = jnp.zeros((targets.shape[0], rows_in.shape[1]), jnp.float32)
    running, unused = lax.scan(accumulate, start_sums, (rows_blocks, keys_blocks))
    return running


def per_device(values, key_ids, heavy_ids, block_offsets, block_counts):
    owners = lax.axis_size("own")
    pairs = lax.axis_size("rep")
    own_index = lax.axis_index("own")
    rep_index = lax.axis_index("rep")
    width = values.shape[1]
    slot_cap = CAP
    padded_values = jnp.concatenate([values, jnp.zeros((slot_cap, width), jnp.float32)], axis=0)
    padded_keys = jnp.concatenate([key_ids, jnp.full((slot_cap,), -1, jnp.int32)], axis=0)
    slot_iota = jnp.arange(slot_cap, dtype=jnp.int32)
    positions = block_offsets[0][:, None] + slot_iota[None, :]
    valid = slot_iota[None, :] < block_counts[0][:, None]
    block_rows = jnp.where(valid[:, :, None], jnp.take(padded_values, positions, axis=0), 0.0)
    block_keys = jnp.where(valid, jnp.take(padded_keys, positions, axis=0), -1)
    half_keys = KEYS_DEV // 2
    owner_base = (jnp.arange(owners, dtype=jnp.int32) * KEYS_DEV)[:, None]
    which_half = jnp.where(block_keys >= 0, (block_keys - owner_base) // half_keys, -1)
    split_rows = jnp.stack(
        [jnp.where((which_half == side)[:, :, None], block_rows, 0.0) for side in range(pairs)],
        axis=0,
    )
    split_keys = jnp.stack(
        [jnp.where(which_half == side, block_keys, -1) for side in range(pairs)], axis=0
    )
    split_rows = split_rows.reshape(pairs * owners, slot_cap, width)
    split_keys = split_keys.reshape(pairs * owners, slot_cap)
    got_rows, got_keys = (
        lax.all_to_all(split_rows, ("rep", "own"), split_axis=0, concat_axis=0, tiled=True),
        lax.all_to_all(split_keys, ("rep", "own"), split_axis=0, concat_axis=0, tiled=True),
    )
    local_keys = jnp.where(
        got_keys >= 0, got_keys - own_index * KEYS_DEV - rep_index * half_keys, -1
    ).reshape(-1)
    owned_half = key_sums(
        got_rows.reshape(-1, width), local_keys, jnp.arange(half_keys, dtype=jnp.int32)
    )
    light_sums = lax.all_gather(owned_half, "rep", axis=0, tiled=True)
    partial_sums = key_sums(values, key_ids, heavy_ids)
    summed_pair = lax.psum(partial_sums, "rep")
    heavy_sums = lax.psum_scatter(summed_pair, "own", scatter_dimension=0, tiled=True)
    return (light_sums, heavy_sums)


def solution(mesh):
    placed = (
        P(("rep", "own"), None),
        P(("rep", "own")),
        P(),
        P(("rep", "own"), None),
        P(("rep", "own"), None),
    )
    return jax.shard_map(
        per_device,
        mesh=mesh,
        in_specs=placed,
        out_specs=(P("own", None), P("own", None)),
        check_vma=False,
    )
```

profile of v0, /device:TPU:0, one launch (start us, length us, event | category | flops | bytes accessed | tf_op | source)
XLA Modules:
  0.0 166.0 jit_solution(6468750620577032743)
XLA Ops:
  8.0 0.7 compare_select_fusion.2
  8.8 0.8 concatenate.6
  9.6 6.1 %gather_fusion = s32[1024]{0:T(1024)S(1)} fusion(s32[8256]{0:T(1024)S(1)} %concatenate.6, s32[1024]{0:T(1024)S(1)} %broadcast_clamp_fusion), kind=kCustom, calls=%fused_computation | custom fusion | bytes 12288 | tf_op jit(solution)/shard_map/jit(_take)/gather | solution.py:44
  15.8 0.1 compare_select_fusion.5
  15.9 0.6 pad_add_fusion
  16.5 7.3 %all-to-all-start = ((s32[32,1,64]{2,1,0:T(1,128)}), s32[32,1,64]{2,1,0:T(1,128)S(1)}, u32[]{:S(2)}, u32[]{:S(2)}) async-start(s32[32,1,64]{2,1,0:T(1,128)} %bitcast.2), calls=%async_computation | async-start | bytes 32768 | tf_op jit(solution)/shard_map/all_to_all | solution.py:59
  23.9 3.7 %concatenate.7 = f32[8256,128]{1,0:T(8,128)} pad(f32[8192,128]{1,0:T(8,128)} %param.7, f32[]{:T(128)} %constant.82.clone.1), padding=0_64x0_0 | pad | bytes 8421380 | tf_op jit(solution)/shard_map/concatenate | solution.py:38
  27.6 5.0 %gather_fusion.1 = f32[1024,128]{1,0:T(8,128)S(1)} fusion(f32[8256,128]{1,0:T(8,128)} %concatenate.7, s32[1024]{0:T(1024)S(1)} %broadcast_clamp_fusion), kind=kCustom, calls=%fused_computation.1 | custom fusion | bytes 1052672 | tf_op jit(solution)/shard_map/jit(_take)/gather | solution.py:43
  32.6 0.1 broadcast_compare_fusion.1
  32.8 0.7 fusion.13
  33.5 1.1 pad_maximum_fusion
  34.6 5.8 %all-to-all-start.1 = ((f32[32,64,128]{2,1,0:T(8,128)}), f32[32,64,128]{2,1,0:T(8,128)S(1)}, u32[]{:S(2)}, u32[]{:S(2)}) async-start(f32[32,64,128]{2,1,0:T(8,128)} %bitcast.4), calls=%async_computation.1 | async-start | bytes 2097152 | tf_op jit(solution)/shard_map/all_to_all | solution.py:58
  40.5 34.5 %while.3 = (s32[]{:T(128)}, f32[2048,128]{1,0:T(8,128)S(1)}, s32[2048]{0:T(1024)S(1)}, s32[4,2048]{1,0:T(4,128)S(1)}, f32[4,2048,128]{2,1,0:T(8,128)}, /*index=5*/s32[]{:T(128)}, s32[]{:T(128)}) while((s32[]{:T(128)}, f32[2048,128]{1,0:T(8,128)S(1)}, s32[2048]{0:T(1024)S(1)}, s32[4,2048]{1,0:T(4,128)S(1)}, ...), condition=%wide.region_1.2_spmd.clone, body=%wide.region_0.1_spmd.clone.sunk | while | flops 6447169536 | bytes 3178599 | solution.py:27
  40.5 8.6 %fusion.34 = f32[2048,128]{1,0:T(8,128)S(1)} fusion(s32[2048]{0:T(1024)S(1)} %bitcast.21, s32[2048]{0:T(1024)S(1)} %get-tuple-element.128, f32[2048,128]{1,0:T(8,128)S(1)} %get-tuple-element.120, f32[4,2048,128]{2,1,0:T(8,128)} %get-tuple-element.130, s32[]{:T(128)S(6)} %copy.9, pred[]{:T(512)S(6)} %compare.29), kind=kOutput, calls=%fused_computation.6.clone.1 | convolution fusion | flops 6447169536 | bytes 3162117 | tf_op jit(solution)/shard_map/while/body/eval_jaxpr/dot_general | solution.py:21
  49.2 8.6 %fusion.34 = f32[2048,128]{1,0:T(8,128)S(1)} fusion(s32[2048]{0:T(1024)S(1)} %bitcast.21, s32[2048]{0:T(1024)S(1)} %get-tuple-element.128, f32[2048,128]{1,0:T(8,128)S(1)} %get-tuple-element.120, f32[4,2048,128]{2,1,0:T(8,128)} %get-tuple-element.130, s32[]{:T(128)S(6)} %copy.9, pred[]{:T(512)S(6)} %compare.29), kind=kOutput, calls=%fused_computation.6.clone.1 | convolution fusion | flops 6447169536 | bytes 3162117 | tf_op jit(solution)/shard_map/while/body/eval_jaxpr/dot_general | solution.py:21
  57.8 8.6 %fusion.34 = f32[2048,128]{1,0:T(8,128)S(1)} fusion(s32[2048]{0:T(1024)S(1)} %bitcast.21, s32[2048]{0:T(1024)S(1)} %get-tuple-element.128, f32[2048,128]{1,0:T(8,128)S(1)} %get-tuple-element.120, f32[4,2048,128]{2,1,0:T(8,128)} %get-tuple-element.130, s32[]{:T(128)S(6)} %copy.9, pred[]{:T(512)S(6)} %compare.29), kind=kOutput, calls=%fused_computation.6.clone.1 | convolution fusion | flops 6447169536 | bytes 3162117 | tf_op jit(solution)/shard_map/while/body/eval_jaxpr/dot_general | solution.py:21
  66.4 8.6 %fusion.34 = f32[2048,128]{1,0:T(8,128)S(1)} fusion(s32[2048]{0:T(1024)S(1)} %bitcast.21, s32[2048]{0:T(1024)S(1)} %get-tuple-element.128, f32[2048,128]{1,0:T(8,128)S(1)} %get-tuple-element.120, f32[4,2048,128]{2,1,0:T(8,128)} %get-tuple-element.130, s32[]{:T(128)S(6)} %copy.9, pred[]{:T(512)S(6)} %compare.29), kind=kOutput, calls=%fused_computation.6.clone.1 | convolution fusion | flops 6447169536 | bytes 3162117 | tf_op jit(solution)/shard_map/while/body/eval_jaxpr/dot_general | solution.py:21
  75.0 1.0 copy-done
  76.0 0.2 all-gather.2.cloned.1.call-start
  76.4 8.6 %fusion.10 = f32[2048,128]{1,0:T(8,128)} fusion(f32[2048,128]{1,0:T(8,128)S(1)} %bitcast.20, s32[2048]{0:T(1024)S(1)} %select_n.222), kind=kOutput, calls=%fused_computation.12 | convolution fusion | flops 6446645248 | bytes 2105344 | tf_op jit(solution)/shard_map/while/body/eval_jaxpr/dot_general | solution.py:21
  85.0 50.0 %reduce-scatter.2.cloned.1.call-done = f32[128,128]{1,0:T(8,128)} async-done(((f32[2048,128]{1,0:T(8,128)}), f32[128,128]{1,0:T(8,128)}) %reduce-scatter.2.cloned.1.call-update) | async-done | bytes 65552 | tf_op jit(solution)/shard_map/reduce_scatter | solution.py:70
  135.0 19.8 %all-reduce.4.cloned.1.call-done = f32[128,128]{1,0:T(8,128)} async-done(((f32[128,128]{1,0:T(8,128)}), f32[128,128]{1,0:T(8,128)}) %all-reduce.4.cloned.1.call-update) | async-done | bytes 65552 | tf_op jit(solution)/shard_map/psum | solution.py:69
  154.9 3.1 %copy.15 = f32[4096,128]{1,0:T(8,128)} copy(f32[4096,128]{1,0:T(8,128)} %all-gather.2.cloned.1.call-done) | data formatting | bytes 4194304
  157.9 0.6 copy.16
  (33 shorter events, 0.6 us)
Async XLA Ops:
  9.6 6.2 %copy-start.3 = (s32[1,16]{1,0:T(1,128)S(1)}, s32[1,16]{1,0:T(1,128)}, u32[]{:S(2)}) copy-start(s32[1,16]{1,0:T(1,128)} %param.10) | copy-start | bytes 196
  9.6 6.2 %copy-start.4 = (s32[1,16]{1,0:T(1,128)S(1)}, s32[1,16]{1,0:T(1,128)}, u32[]{:S(2)}) copy-start(s32[1,16]{1,0:T(1,128)} %param.11) | copy-start | bytes 196
  16.5 18.1 %all-to-all-start = ((s32[32,1,64]{2,1,0:T(1,128)}), s32[32,1,64]{2,1,0:T(1,128)S(1)}, u32[]{:S(2)}, u32[]{:S(2)}) async-start(s32[32,1,64]{2,1,0:T(1,128)} %bitcast.2), calls=%async_computation | async-start | bytes 32768 | tf_op jit(solution)/shard_map/all_to_all | solution.py:59
  27.6 6.9 %copy-start.1 = (s32[8192]{0:T(1024)S(1)}, s32[8192]{0:T(1024)}, u32[]{:S(2)}) copy-start(s32[8192]{0:T(1024)} %param.8) | copy-start | bytes 98308
  27.6 12.9 %copy-start.5 = (s32[2048]{0:T(1024)S(1)}, s32[2048]{0:T(1024)}, u32[]{:S(2)}) copy-start(s32[2048]{0:T(1024)} %param.9) | copy-start | bytes 24580
  34.6 41.8 %all-to-all-start.1 = ((f32[32,64,128]{2,1,0:T(8,128)}), f32[32,64,128]{2,1,0:T(8,128)S(1)}, u32[]{:S(2)}, u32[]{:S(2)}) async-start(f32[32,64,128]{2,1,0:T(8,128)} %bitcast.4), calls=%async_computation.1 | async-start | bytes 2097152 | tf_op jit(solution)/shard_map/all_to_all | solution.py:58
  40.4 94.5 %reduce-scatter.2.cloned.1.call-start = ((), (), s32[]{:S(2)}) async-start(), calls=%async_computation.4 | async-start | bytes 1114112 | tf_op jit(solution)/shard_map/reduce_scatter | solution.py:70
  75.0 1.0 copy-start
  76.0 59.1 %all-gather.2.cloned.1.call-start = ((), (), s32[]{:S(2)}) async-start(), calls=%async_computation.3 | async-start | bytes 3145728 | tf_op jit(solution)/shard_map/all_gather | solution.py:67
  85.0 69.9 %all-reduce.4.cloned.1.call-start = ((), (), s32[]{:S(2)}) async-start(), calls=%async_computation.5 | async-start | bytes 131072 | tf_op jit(solution)/shard_map/psum | solution.py:69
  154.9 3.1 %copy-start.2 = (f32[128,128]{1,0:T(8,128)S(1)}, f32[128,128]{1,0:T(8,128)}, u32[]{:S(2)}) copy-start(f32[128,128]{1,0:T(8,128)} %all-reduce.4.cloned.1.call-done) | copy-start | bytes 196612
Sparse Core Ops, SparseCore 0:
  76.1 58.8 reduce-scatter.1
Sparse Core Ops, SparseCore 1:
  85.0 34.2 all-gather.1
  135.1 19.7 all-reduce.3
where the time goes:
time: 167 us; the launch traced here: 166 us
  waiting for transfers between devices  69.9 us (42%)
  matrix products  42.9 us (26%)
  local copies, waits for them, and re-layouts  20.7 us (12%)
  between operations  15.6 us (9%)
  starting transfers between devices  13.5 us (8%)
  other arithmetic  3.39 us (2%)
    reduce_scatter x1, waiting for transfers between devices, per_device(): lax.psum_scatter(summed_pair, 'own', scatter_dimension=0, tiled=True)  50 us
    dot_general x5, matrix products, accumulate(): jnp.dot(onehot, rows_piece, precision=lax.Precision.HIGHEST, preferred_el...  42.9 us
    psum x1, waiting for transfers between devices, per_device(): summed_pair = lax.psum(partial_sums, 'rep')  19.8 us
    all_to_all x1, starting transfers between devices, per_device(): lax.all_to_all(split_keys, ('rep', 'own'), split_axis=0, concat_axis=0, t...  7.33 us
    gather x3, local copies, waits for them, and re-layouts, per_device(): block_keys = jnp.where(valid, jnp.take(padded_keys, positions, axis=0), -1)  6.28 us
    all_to_all x1, starting transfers between devices, per_device(): lax.all_to_all(split_rows, ('rep', 'own'), split_axis=0, concat_axis=0, t...  5.84 us
    gather x1, local copies, waits for them, and re-layouts, per_device(): jnp.take(padded_values, positions, axis=0)  5 us
    unnamed x14, local copies, waits for them, and re-layouts  4.68 us
  transfers between devices with their start and end apart: 5, of which 2 were waited for; matrix products, arithmetic and copies ran while one was open for 32% of the time, Pallas kernels for 0%

commit v1 on v0

--- a/solution.py
+++ b/solution.py
@@ -1,11 +1,21 @@
+import functools
 import math
 import jax
 import jax.numpy as jnp
 from jax import lax
 from jax.sharding import PartitionSpec as P
+from jax.lax import ppermute
 
 KEYS_DEV = 4096
 CAP = 64
+
+
+def _press_knots(packet, bus_axis):
+    mid_arr = packet + ppermute(packet, bus_axis, [(0, 1), (1, 0)])
+    return mid_arr
+
+
+run_the_surface = functools.partial(_press_knots, bus_axis="rep")
 
 
 def key_sums(rows_in, row_keys, targets):
@@ -66,7 +76,7 @@
     )
     light_sums = lax.all_gather(owned_half, "rep", axis=0, tiled=True)
     partial_sums = key_sums(values, key_ids, heavy_ids)
-    summed_pair = lax.psum(partial_sums, "rep")
+    summed_pair = run_the_surface(partial_sums)
     heavy_sums = lax.psum_scatter(summed_pair, "own", scatter_dimension=0, tiled=True)
     return (light_sums, heavy_sums)
 

time: 167 us -> 203 us (1.22)
  waiting for transfers between devices: 69.9 us -> 106 us
    all_to_all x1, waiting for transfers between devices: 0.01 us -> 26.9 us  [per_device(): lax.all_to_all(split_rows, ('rep', 'own'), split_axis=0, concat_axis=0, t...]
    ppermute x0 -> x1, waiting for transfers between devices: none -> 23.7 us  [_press_knots(): mid_arr = packet + ppermute(packet, bus_axis, [(0, 1), (1, 0)])]
    psum x1 -> x0, waiting for transfers between devices: 19.8 us -> none  [per_device(): summed_pair = lax.psum(partial_sums, 'rep')]
    reduce_scatter x1, waiting for transfers between devices: 50 us -> 55.3 us  [per_device(): lax.psum_scatter(summed_pair, 'own', scatter_dimension=0, tiled=True)]
    unnamed x14 -> x9, local copies, waits for them, and re-layouts: 4.68 us -> 3.06 us
  transfers between devices with their start and end apart: 5 -> 5, of which waited for: 2 -> 3; matrix products, arithmetic and copies ran while one was open for 32% -> 23% of each run, Pallas kernels for 0% -> 0%
where the time goes in v1:
time: 203 us; the launch traced here: 202 us
  waiting for transfers between devices  106 us (52%)
  matrix products  42.9 us (21%)
  local copies, waits for them, and re-layouts  19 us (9%)
  between operations  15.6 us (8%)
  starting transfers between devices  14.3 us (7%)
  other arithmetic  4.47 us (2%)
    reduce_scatter x1, waiting for transfers between devices, per_device(): lax.psum_scatter(summed_pair, 'own', scatter_dimension=0, tiled=True)  55.3 us
    dot_general x5, matrix products, accumulate(): jnp.dot(onehot, rows_piece, precision=lax.Precision.HIGHEST, preferred_el...  42.9 us
    all_to_all x1, waiting for transfers between devices, per_device(): lax.all_to_all(split_rows, ('rep', 'own'), split_axis=0, concat_axis=0, t...  26.9 us
    ppermute x1, waiting for transfers between devices, _press_knots(): mid_arr = packet + ppermute(packet, bus_axis, [(0, 1), (1, 0)])  23.7 us
    all_to_all x1, starting transfers between devices, per_device(): lax.all_to_all(split_keys, ('rep', 'own'), split_axis=0, concat_axis=0, t...  7.33 us
    gather x3, local copies, waits for them, and re-layouts, per_device(): block_keys = jnp.where(valid, jnp.take(padded_keys, positions, axis=0), -1)  6.28 us
    all_to_all x1, starting transfers between devices, per_device(): lax.all_to_all(split_rows, ('rep', 'own'), split_axis=0, concat_axis=0, t...  5.83 us
    gather x1, local copies, waits for them, and re-layouts, per_device(): jnp.take(padded_values, positions, axis=0)  5.01 us
  transfers between devices with their start and end apart: 5, of which 3 were waited for; matrix products, arithmetic and copies ran while one was open for 23% of the time, Pallas kernels for 0%

profile of v1, /device:TPU:0, one launch (start us, length us, event | category | flops | bytes accessed | tf_op | source)
XLA Modules:
  0.0 202.5 jit_solution(698761218617572069)
XLA Ops:
  8.0 0.7 compare_select_fusion.2
  8.8 0.8 concatenate.6
  9.6 6.1 %gather_fusion = s32[1024]{0:T(1024)S(1)} fusion(s32[8256]{0:T(1024)S(1)} %concatenate.6, s32[1024]{0:T(1024)S(1)} %broadcast_clamp_fusion), kind=kCustom, calls=%fused_computation | custom fusion | bytes 12288 | tf_op jit(solution)/shard_map/jit(_take)/gather | solution.py:54
  15.9 0.6 pad_add_fusion
  16.5 7.3 %all-to-all-start = ((s32[32,1,64]{2,1,0:T(1,128)}), s32[32,1,64]{2,1,0:T(1,128)S(1)}, u32[]{:S(2)}, u32[]{:S(2)}) async-start(s32[32,1,64]{2,1,0:T(1,128)} %bitcast.2), calls=%async_computation | async-start | bytes 32768 | tf_op jit(solution)/shard_map/all_to_all | solution.py:69
  23.9 0.1 broadcast_compare_fusion.1
  24.0 3.7 %concatenate.7 = f32[8256,128]{1,0:T(8,128)} pad(f32[8192,128]{1,0:T(8,128)} %param.7, f32[]{:T(128)} %constant.82.clone.1), padding=0_64x0_0 | pad | bytes 8421380 | tf_op jit(solution)/shard_map/concatenate | solution.py:48
  27.7 5.0 %gather_fusion.1 = f32[1024,128]{1,0:T(8,128)S(1)} fusion(f32[8256,128]{1,0:T(8,128)} %concatenate.7, s32[1024]{0:T(1024)S(1)} %broadcast_clamp_fusion), kind=kCustom, calls=%fused_computation.1 | custom fusion | bytes 1052672 | tf_op jit(solution)/shard_map/jit(_take)/gather | solution.py:53
  32.7 0.7 fusion.13
  33.5 1.1 pad_maximum_fusion
  34.6 5.8 %all-to-all-start.1 = ((f32[32,64,128]{2,1,0:T(8,128)}), f32[32,64,128]{2,1,0:T(8,128)S(1)}, u32[]{:S(2)}, u32[]{:S(2)}) async-start(f32[32,64,128]{2,1,0:T(8,128)} %bitcast.4), calls=%async_computation.1 | async-start | bytes 2097152 | tf_op jit(solution)/shard_map/all_to_all | solution.py:68
  40.6 26.9 %all-to-all-done.1 = f32[32,64,128]{2,1,0:T(8,128)S(1)} async-done(((f32[32,64,128]{2,1,0:T(8,128)}), f32[32,64,128]{2,1,0:T(8,128)S(1)}, u32[]{:S(2)}, u32[]{:S(2)}) %all-to-all-start.1) | async-done | bytes 1048608 | tf_op jit(solution)/shard_map/all_to_all | solution.py:68
  67.6 8.6 %fusion.10 = f32[2048,128]{1,0:T(8,128)} fusion(f32[2048,128]{1,0:T(8,128)S(1)} %bitcast.20, s32[2048]{0:T(1024)S(1)} %select_n.222), kind=kOutput, calls=%fused_computation.12 | convolution fusion | flops 6446645248 | bytes 2105344 | tf_op jit(solution)/shard_map/while/body/eval_jaxpr/dot_general | solution.py:31
  76.2 0.2 reduce-scatter.2.cloned.1.call-start
  76.4 34.5 %while.3 = (s32[]{:T(128)}, f32[2048,128]{1,0:T(8,128)S(1)}, s32[2048]{0:T(1024)S(1)}, s32[4,2048]{1,0:T(4,128)S(1)}, f32[4,2048,128]{2,1,0:T(8,128)}, /*index=5*/s32[]{:T(128)}, s32[]{:T(128)}) while((s32[]{:T(128)}, f32[2048,128]{1,0:T(8,128)S(1)}, s32[2048]{0:T(1024)S(1)}, s32[4,2048]{1,0:T(4,128)S(1)}, ...), condition=%wide.region_1.2_spmd.clone, body=%wide.region_0.1_spmd.clone.sunk | while | flops 6447169536 | bytes 3178599 | solution.py:37
  76.4 8.6 %fusion.34 = f32[2048,128]{1,0:T(8,128)S(1)} fusion(s32[2048]{0:T(1024)S(1)} %bitcast.21, s32[2048]{0:T(1024)S(1)} %get-tuple-element.128, f32[2048,128]{1,0:T(8,128)S(1)} %get-tuple-element.120, f32[4,2048,128]{2,1,0:T(8,128)} %get-tuple-element.130, s32[]{:T(128)S(6)} %copy.9, pred[]{:T(512)S(6)} %compare.29), kind=kOutput, calls=%fused_computation.6.clone.1 | convolution fusion | flops 6447169536 | bytes 3162117 | tf_op jit(solution)/shard_map/while/body/eval_jaxpr/dot_general | solution.py:31
  85.1 8.6 %fusion.34 = f32[2048,128]{1,0:T(8,128)S(1)} fusion(s32[2048]{0:T(1024)S(1)} %bitcast.21, s32[2048]{0:T(1024)S(1)} %get-tuple-element.128, f32[2048,128]{1,0:T(8,128)S(1)} %get-tuple-element.120, f32[4,2048,128]{2,1,0:T(8,128)} %get-tuple-element.130, s32[]{:T(128)S(6)} %copy.9, pred[]{:T(512)S(6)} %compare.29), kind=kOutput, calls=%fused_computation.6.clone.1 | convolution fusion | flops 6447169536 | bytes 3162117 | tf_op jit(solution)/shard_map/while/body/eval_jaxpr/dot_general | solution.py:31
  93.7 8.6 %fusion.34 = f32[2048,128]{1,0:T(8,128)S(1)} fusion(s32[2048]{0:T(1024)S(1)} %bitcast.21, s32[2048]{0:T(1024)S(1)} %get-tuple-element.128, f32[2048,128]{1,0:T(8,128)S(1)} %get-tuple-element.120, f32[4,2048,128]{2,1,0:T(8,128)} %get-tuple-element.130, s32[]{:T(128)S(6)} %copy.9, pred[]{:T(512)S(6)} %compare.29), kind=kOutput, calls=%fused_computation.6.clone.1 | convolution fusion | flops 6447169536 | bytes 3162117 | tf_op jit(solution)/shard_map/while/body/eval_jaxpr/dot_general | solution.py:31
  102.3 8.6 %fusion.34 = f32[2048,128]{1,0:T(8,128)S(1)} fusion(s32[2048]{0:T(1024)S(1)} %bitcast.21, s32[2048]{0:T(1024)S(1)} %get-tuple-element.128, f32[2048,128]{1,0:T(8,128)S(1)} %get-tuple-element.120, f32[4,2048,128]{2,1,0:T(8,128)} %get-tuple-element.130, s32[]{:T(128)S(6)} %copy.9, pred[]{:T(512)S(6)} %compare.29), kind=kOutput, calls=%fused_computation.6.clone.1 | convolution fusion | flops 6447169536 | bytes 3162117 | tf_op jit(solution)/shard_map/while/body/eval_jaxpr/dot_general | solution.py:31
  110.9 0.9 collective-permute-start
  111.9 23.7 %collective-permute-done = f32[2048,128]{1,0:T(8,128)S(1)} collective-permute-done((f32[2048,128]{1,0:T(8,128)S(1)}, f32[2048,128]{1,0:T(8,128)S(1)}, u32[]{:S(2)}, u32[]{:S(2)}) %collective-permute-start) | collective-permute-done | bytes 1048608 | tf_op jit(solution)/shard_map/ppermute | solution.py:14
  135.5 1.1 add.141
  136.7 55.3 %reduce-scatter.2.cloned.1.call-done = f32[128,128]{1,0:T(8,128)} async-done(((f32[2048,128]{1,0:T(8,128)}), f32[128,128]{1,0:T(8,128)}) %reduce-scatter.2.cloned.1.call-update) | async-done | bytes 65552 | tf_op jit(solution)/shard_map/reduce_scatter | solution.py:80
  192.0 3.0 %copy.14 = f32[4096,128]{1,0:T(8,128)} copy(f32[4096,128]{1,0:T(8,128)} %all-gather.2.cloned.1.call-done) | data formatting | bytes 4194304
  (28 shorter events, 0.6 us)
Async XLA Ops:
  9.6 6.2 %copy-start.1 = (s32[1,16]{1,0:T(1,128)S(1)}, s32[1,16]{1,0:T(1,128)}, u32[]{:S(2)}) copy-start(s32[1,16]{1,0:T(1,128)} %param.10) | copy-start | bytes 196
  9.6 6.2 %copy-start.2 = (s32[1,16]{1,0:T(1,128)S(1)}, s32[1,16]{1,0:T(1,128)}, u32[]{:S(2)}) copy-start(s32[1,16]{1,0:T(1,128)} %param.11) | copy-start | bytes 196
  16.5 18.0 %all-to-all-start = ((s32[32,1,64]{2,1,0:T(1,128)}), s32[32,1,64]{2,1,0:T(1,128)S(1)}, u32[]{:S(2)}, u32[]{:S(2)}) async-start(s32[32,1,64]{2,1,0:T(1,128)} %bitcast.2), calls=%async_computation | async-start | bytes 32768 | tf_op jit(solution)/shard_map/all_to_all | solution.py:69
  27.7 12.7 %copy-start = (s32[8192]{0:T(1024)S(1)}, s32[8192]{0:T(1024)}, u32[]{:S(2)}) copy-start(s32[8192]{0:T(1024)} %param.8) | copy-start | bytes 98308
  34.6 33.0 %all-to-all-start.1 = ((f32[32,64,128]{2,1,0:T(8,128)}), f32[32,64,128]{2,1,0:T(8,128)S(1)}, u32[]{:S(2)}, u32[]{:S(2)}) async-start(f32[32,64,128]{2,1,0:T(8,128)} %bitcast.4), calls=%async_computation.1 | async-start | bytes 2097152 | tf_op jit(solution)/shard_map/all_to_all | solution.py:68
  40.4 96.3 %all-gather.2.cloned.1.call-start = ((), (), s32[]{:S(2)}) async-start(), calls=%async_computation.3 | async-start | bytes 3145728 | tf_op jit(solution)/shard_map/all_gather | solution.py:77
  67.6 8.8 %copy-start.3 = (s32[2048]{0:T(1024)S(1)}, s32[2048]{0:T(1024)}, u32[]{:S(2)}) copy-start(s32[2048]{0:T(1024)} %param.9) | copy-start | bytes 24580
  76.2 115.8 %reduce-scatter.2.cloned.1.call-start = ((), (), s32[]{:S(2)}) async-start(), calls=%async_computation.4 | async-start | bytes 1114112 | tf_op jit(solution)/shard_map/reduce_scatter | solution.py:80
  110.9 24.6 %collective-permute-start = (f32[2048,128]{1,0:T(8,128)S(1)}, f32[2048,128]{1,0:T(8,128)S(1)}, u32[]{:S(2)}, u32[]{:S(2)}) collective-permute-start(f32[2048,128]{1,0:T(8,128)S(1)} %get-tuple-element.44), channel_id=1, source_target_pairs={{0,16},{16,0},{1,17},{17,1},{2,18},{18,2},{3,19},{19,3},{4,20},{20... | collective-permute-start | bytes 3145736 | tf_op jit(solution)/shard_map/ppermute | solution.py:14
Sparse Core Ops, SparseCore 0:
  76.3 30.3 all-gather.1
Sparse Core Ops, SparseCore 1:
  136.7 55.2 reduce-scatter.1
